TPU v7x, 256 devices: a 2x2x32 block of a 4x8x32 slice. The times are simulated.
256 devices in a mesh: replica: 4 (over x, y), tp: 32 (over z), sub: 2 (over core).
Axes of the slice: x: 2, y: 2, z: 32, core: 2. Of those that a mesh axis runs over, the one named last changes fastest.
The devices are a block of a 4x8x32 slice.
Arguments:
- hidden_in: bfloat16 [16, 8192], P('replica'), parts along dimension 0, may hold values from -6 to 6
- norm_gain: float32 [32768], P('replica'), parts along dimension 0, may hold values from 0.1 to 1.9
- wqkv_old: bfloat16 [128, 2, 1280, 1024], P(('replica', 'tp'), 'sub'), parts along dimension 0, may hold values from -0.1875 to 0.1875
- wo: bfloat16 [32768, 8192], P(('replica', 'tp', 'sub')), parts along dimension 0, may hold values from -0.0625 to 0.0625
- key_cache: bfloat16 [16, 4096, 1024], P('replica', ('tp', 'sub')), parts along dimension 0, may hold values from -240 to 240
- value_cache: bfloat16 [16, 4096, 1024], P('replica', ('tp', 'sub')), parts along dimension 0, may hold values from -6 to 6
- lengths: int32 [16], P('replica'), parts along dimension 0, may hold values from 1 to 4096
- section_order: int32 [64], P('replica'), parts along dimension 0, may hold values from 0 to 15, each once
Outputs:
- mixed_out: bfloat16 [16, 8192], P('replica'), parts along dimension 0
- wqkv_new: bfloat16 [128, 2, 160, 8192], P(('replica', 'tp'), 'sub'), parts along dimension 0
There are 4 independent parts, one for each index of `replica`. A program takes and returns all parts, laid end to end along the dimension named above; each array names one. Nothing has to cross between parts.
Inputs may be any that keep to these rules, and one draw needn't show every extreme that they name: `section_order`: each input row block appears once. The new token's position is lengths[b].
All inputs are finite; a program needn't handle non-finite values.
Results may differ from a plain program's by a relative error of at most 0.0085.
The roundings to bfloat16 on the way count: a program that leaves them out, or rounds other values in their place, can miss the bound.
Values may be sent and summed in bfloat16 or wider, within the bound.
A program may use at most 64 MiB of HBM per device.

v0:
```python
import functools
import math

import jax
import jax.numpy as jnp
import numpy as np
from jax import lax
from jax.experimental import pallas as pl
from jax.experimental.pallas import tpu as pltpu
from jax.sharding import PartitionSpec as P

HEADS = 64
KV_HEADS = 8
HEAD_DIM = 128
ROW_BLOCKS = 16
NEAR = 4
SECTIONS = 8
FEEDS = (0, 0, 0, 1, 1, 1, 1, 1)
HIGH_ROWS = 72
STEP_ROWS = 16

FIRST = (4, 2, 1, 0)
MESH = pl.DeviceIdType.MESH
F32 = jnp.float32
BF16 = jnp.bfloat16


def nt_dot(x, y):
    return lax.dot_general(x, y, (((1,), (1,)), ((), ())), preferred_element_type=F32)


def spread(x):
    lane = lax.broadcasted_iota(jnp.int32, x.shape, 1)
    row = lax.broadcasted_iota(jnp.int32, x.shape, 0)
    return jnp.max(jnp.where((lane >> 5) == row, x, -3e38), -1, keepdims=True)


def merged(tiles, seqs):
    tops, totals = [], []
    low = (lax.broadcasted_iota(jnp.int32, (seqs, 128), 1) & 16) == 0
    for tile in tiles:
        stat = jnp.broadcast_to(tile[seqs : seqs + 1, :], (seqs, 128))
        tops.append(jnp.where(low, stat, pltpu.roll(stat, 16, 1)))
        totals.append(jnp.where(low, pltpu.roll(stat, 112, 1), stat))
    best = functools.reduce(jnp.maximum, tops)
    mix, total = None, None
    for tile, top, s in zip(tiles, tops, totals):
        f = jnp.exp(top - best)
        m = tile[0:seqs, :] * spread(f)
        mix = m if mix is None else mix + m
        total = s * f if total is None else total + s * f
    return mix, best, total


def main_kernel(
    hid_in, gain_in, table_in, lengths, order, w, wo, kc, vc,
    recv, g_out,
    hid, gain, table, w_v, wo_v, k_v, v_v, nrm, p_tx, p_rx, q_tx, q_all, rows, state, a_rx1, a_rx2,
    a_tx, a_rx3, heads, part, o_rx1, o_rx2, o_tx, o_rx3, g_all,
    load_sem, big_s, big_r, far_s, far_r, loc_s, loc_r, duo_s, duo_r, known_lo, known_hi,
):
    count = lax.axis_size("tp")
    t = lax.axis_index("tp")
    s = lax.axis_index("sub")
    a = t // NEAR
    c = t % NEAR
    seqs, width = hid_in.shape
    cols = recv.shape[1]
    leads, helps = s == 1, s == 0

    def far_id(k):
        return {"tp": lax.rem(t + NEAR * k, count)}

    def loc_id(d):
        return {"tp": lax.rem(t + d + count, count)}

    duo_id = {"sub": 1 - s}

    barrier = pltpu.get_barrier_semaphore()
    greeted = [loc_id(d) for d in (1, -1, 2, -2, NEAR, -NEAR)] + [duo_id]
    for target in greeted:
        pl.semaphore_signal(barrier, inc=1, device_id=target, device_id_type=MESH)

    loads = [
        pltpu.make_async_copy(src, dst, load_sem.at[i])
        for i, (src, dst) in enumerate(
            (
                (w, w_v),
                (kc, k_v),
                (vc, v_v),
                (wo, wo_v),
                (hid_in, hid),
                (gain_in, gain),
                (table_in, table),
            )
        )
    ]
    for i in (4, 5, 0):
        loads[i].start()
    pl.semaphore_wait(barrier, len(greeted))

    def piece(k, row, height):
        b = lax.rem(a + k, SECTIONS)
        first = pl.multiple_of(b * cols + row, 8)
        return pltpu.make_async_remote_copy(
            src_ref=w.at[pl.ds(first, height), :],
            dst_ref=recv.at[a, pl.ds(row, height), :],
            send_sem=big_s.at[k],
            recv_sem=big_r.at[SECTIONS - k],
            device_id=far_id(k),
            device_id_type=MESH,
        )

    sent = {}

    def stream(core, ks, n):
        ks = [k for k in ks if sent.get((core, k), 0) < cols]
        n = min([n] + [(cols - sent.get((core, k), 0)) // STEP_ROWS for k in ks])
        if not ks or n == 0:
            return
        starts = {k: sent.get((core, k), 0) for k in ks}

        def body(i, carry):
            for k in ks:
                piece(k, pl.multiple_of(starts[k] + i * STEP_ROWS, 8), STEP_ROWS).start()
            return carry

        @pl.when(s == core)
        def _():
            lax.fori_loop(0, n, body, 0)

        for k in ks:
            sent[core, k] = starts[k] + n * STEP_ROWS

    everyone = (4, 3, 5, 2, 6, 1, 7)
    feeds = iter(FEEDS)

    def stream_rest(core):
        while any(sent.get((core, k), 0) < cols for k in everyone):
            stream(core, everyone, cols // STEP_ROWS)

    def tell(stage):
        pl.semaphore_signal(known_lo.at[stage], inc=1, device_id=far_id(1), device_id_type=MESH)
        pl.semaphore_signal(
            known_hi.at[stage], inc=1, device_id=far_id(SECTIONS - 1), device_id_type=MESH
        )

    def hear(stage):
        pl.semaphore_wait(known_lo.at[stage], 1)
        pl.semaphore_wait(known_hi.at[stage], 1)

    tell(0)
    stream(0, (1, 7), FIRST[0])
    stream(1, (1, 7), FIRST[3])
    for i in (6, 1, 2, 3):
        loads[i].start()
    hear(0)
    tell(1)
    stream(0, (2, 6), FIRST[1])

    def remote(src, dst, send_sem, recv_sem, target):
        return pltpu.make_async_remote_copy(
            src_ref=src,
            dst_ref=dst,
            send_sem=send_sem,
            recv_sem=recv_sem,
            device_id=target,
            device_id_type=MESH,
        )

    def far_copies(phase, src, dst):
        return [
            remote(
                src(lax.rem(a + k, SECTIONS)),
                dst,
                far_s.at[phase, k],
                far_r.at[phase, SECTIONS - k],
                far_id(k),
            )
            for k in (4, 3, 5, 2, 6, 1, 7)
        ]

    def loc_copies(phase, src, dst):
        out = []
        for i, (d, h) in enumerate(((1, None), (-1, None), (2, 0), (-2, 1))):
            place = lax.rem(c + d + NEAR, NEAR)
            sems = loc_s.at[phase, i], loc_r.at[phase, i]
            out.append(remote(src(place, h), dst(min(i, 2), h), *sems, loc_id(d)))
        return out

    def part_of(ref, at, size, h):
        if h is None:
            return ref.at[pl.ds(at, size)]
        return ref.at[pl.ds(at + h * (size // 2), size // 2)]

    def duo_copy(phase, src, dst):
        return remote(src, dst, duo_s.at[phase], duo_r.at[phase], duo_id)

    def start(copies):
        for copy in copies:
            copy.start()

    def wait(copies):
        for copy in copies:
            copy.wait()

    loads[4].wait()
    loads[5].wait()
    block = nrm.shape[2]
    squares = jnp.zeros((seqs, 1), F32)
    for i in range(ROW_BLOCKS):
        x = hid[:, i * block : (i + 1) * block].astype(F32)
        squares = squares + jnp.sum(x * x, -1, keepdims=True)
    factor = lax.rsqrt(squares * (1.0 / width) + 1e-05)
    for i in range(ROW_BLOCKS):
        x = hid[:, i * block : (i + 1) * block].astype(F32)
        y = (x * factor * gain[:, i * block : (i + 1) * block]).astype(BF16)
        nrm[i] = y.astype(F32)

    hear(1)
    tell(2)
    stream(0, (3, 5), FIRST[2])

    per_section = ROW_BLOCKS // SECTIONS
    mine = [nrm[order[per_section * a + i]].astype(BF16) for i in range(per_section)]
    normed = jnp.concatenate(mine, -1)
    loads[0].wait()
    units = w.shape[0] // HEAD_DIM
    half = units // 2
    for u in range(units):
        y = nt_dot(normed, w_v[u * HEAD_DIM : (u + 1) * HEAD_DIM, :])
        for b in range(seqs):
            p_tx[2 * b + u // half, s, u % half : u % half + 1, :] = y[b : b + 1, :]
    own_rows = pl.ds(pl.multiple_of(a * cols, 8), cols)
    keep = pltpu.make_async_copy(w.at[own_rows, :], recv.at[a], load_sem.at[7])
    keep.start()

    hear(2)
    def own_q(_, h):
        return part_of(q_all.at[c], 0, SECTIONS, h)

    def own_g(_, h):
        return part_of(g_all.at[c], 0, SECTIONS, h)

    give_p = duo_copy(0, p_tx.at[:, 0], p_tx.at[:, 0])
    give_q = duo_copy(1, q_all, q_all)

    @pl.when(helps)
    def _():
        give_p.start()

    stream_rest(0)

    @pl.when(helps)
    def _():
        give_p.wait_send()
        give_q.wait_recv()

    @pl.when(leads)
    def _():
        give_p.wait_recv()
        copies = far_copies(0, lambda b: p_tx.at[b], p_rx.at[a])
        start(copies)
        stream(1, everyone, next(feeds))
        p_rx[a] = p_tx[a]
        wait(copies)
        total = p_rx[0]
        for i in range(1, SECTIONS):
            total = total + p_rx[i]
        q_tx[:, 0:half, :] = total.astype(BF16)
        q_all[c, a, :, 0:half, :] = total.astype(BF16)

        copies = far_copies(1, lambda b: q_tx, q_all.at[c, a])
        start(copies)
        stream(1, everyone, next(feeds))
        wait(copies)

        copies = loc_copies(0, own_q, own_q)
        start(copies)
        stream(1, everyone, next(feeds))
        wait(copies)
        give_q.start()
        give_q.wait_send()

    rotated = HEADS + KV_HEADS
    loads[6].wait()
    low = lax.broadcasted_iota(jnp.int32, (1, HEAD_DIM), 1) < 64

    def halves_of(row):
        turned = pltpu.roll(row, 64, 1)
        return jnp.where(low, row, turned), jnp.where(low, turned, row)

    for b in range(seqs):
        cos_hi, sin_hi = halves_of(table[pl.ds(lengths[b] // 64, 1), :])
        cos_lo, sin_lo = halves_of(table[pl.ds(HIGH_ROWS + lengths[b] % 64, 1), :])
        cosine = cos_hi * cos_lo - sin_hi * sin_lo
        sine = sin_hi * cos_lo + cos_hi * sin_lo
        sine = jnp.where(low, -sine, sine)
        for j in range(2 * SECTIONS):
            rank = j // 2
            rows[b, j * half : (j + 1) * half, :] = q_all[rank // 2, 2 * b + j % 2, rank % 2][
                :half
            ].astype(F32)
        x = rows[b, :rotated, :]
        x = x * cosine + pltpu.roll(x, 64, 1) * sine
        rows[b, :rotated, :] = x.astype(BF16).astype(F32)

    for copy in loads[1:3]:
        copy.wait()
    groups = HEADS // KV_HEADS
    inverse = 1.0 / math.sqrt(HEAD_DIM)
    pos_count = k_v.shape[1]
    first = (2 * t + s) * pos_count

    def one_sequence(b, carry):
        position = first + lax.broadcasted_iota(jnp.int32, (groups, pos_count), 1)
        usable = position < lengths[b]
        lane = lax.broadcasted_iota(jnp.int32, (groups, HEAD_DIM), 1)
        stats = []
        for k in range(KV_HEADS):
            lanes = slice(k * HEAD_DIM, (k + 1) * HEAD_DIM)
            q = rows[b, k * groups : (k + 1) * groups, :].astype(BF16)
            scores = nt_dot(q, k_v[b, :, lanes]) * inverse
            top = jnp.max(jnp.where(usable, scores, -1e30), -1, keepdims=True)
            weights = jnp.exp(jnp.where(usable, scores - top, -1e30))
            total = jnp.sum(weights, -1, keepdims=True)
            mix = jnp.dot(weights.astype(BF16), v_v[b, :, lanes], preferred_element_type=F32)
            stat = jnp.where((lane & 16) == 0, top, total)
            stats.append(jnp.where((lane >> 5) == b, stat, carry[k]))
            for g in range(groups):
                state[g // 2, k, g % 2, pl.ds(b, 1), :] = mix[g : g + 1, :]
        return tuple(stats)

    nothing = jnp.zeros((groups, HEAD_DIM), F32)
    stats = lax.fori_loop(0, seqs, one_sequence, (nothing,) * KV_HEADS)
    for k in range(KV_HEADS):
        for g in range(groups):
            state[g // 2, k, g % 2, seqs : seqs + 1, :] = stats[k][g : g + 1, :]

    def put(ref, part):
        mix, best, total = part
        low16 = (lax.broadcasted_iota(jnp.int32, best.shape, 1) & 16) == 0
        ref[0:seqs, :] = mix
        ref[seqs : seqs + 1, :] = jnp.where(low16, best, total)[0:1, :]

    give_state = duo_copy(2, state, a_rx1)
    give_head = duo_copy(3, heads.at[0], heads.at[0])

    @pl.when(helps)
    def _():
        give_state.start()
        give_state.wait_send()
        give_head.wait_recv()

    @pl.when(leads)
    def _():
        give_state.wait_recv()

        def merge_duo(i, carry):
            u, v = i // SECTIONS, i % SECTIONS
            for e in range(2):
                put(a_tx.at[u, v, e], merged([state[u, v, e], a_rx1[u, v, e]], seqs))
            return carry

        lax.fori_loop(0, NEAR * SECTIONS, merge_duo, 0, unroll=2)

        copies = loc_copies(
            1,
            lambda place, h: part_of(a_tx.at[place], 0, SECTIONS, h),
            lambda i, h: part_of(a_rx2.at[i], 0, SECTIONS, h),
        )
        start(copies)
        stream(1, everyone, next(feeds))
        a_rx2[3] = a_tx[c]
        wait(copies)

        def merge_loc(v, carry):
            for e in range(2):
                put(state.at[0, v, e], merged([a_rx2[i, v, e] for i in range(NEAR)], seqs))
            return carry

        lax.fori_loop(0, SECTIONS, merge_loc, 0)

        copies = far_copies(2, lambda b: state.at[0, b], a_rx3.at[a])
        start(copies)
        stream(1, everyone, next(feeds))
        a_rx3[a] = state[0, a]
        wait(copies)

        def head_rows(at):
            return jnp.concatenate([rows[b, pl.ds(at, 1), :] for b in range(seqs)], 0)

        for e in range(2):
            mix, best, total = merged([a_rx3[i, e] for i in range(SECTIONS)], seqs)
            best, total = spread(best), spread(total)
            head = groups * a + 2 * c + e
            products = head_rows(head) * head_rows(HEADS + a)
            own_score = jnp.sum(products, -1, keepdims=True) * inverse
            highest = jnp.maximum(best, own_score)
            old_scale = jnp.exp(best - highest)
            own_weight = jnp.exp(own_score - highest)
            numerator = mix * old_scale + own_weight * head_rows(rotated + a)
            denominator = total * old_scale + own_weight
            heads[e] = (numerator / denominator).astype(BF16).astype(F32)
        give_head.start()
        give_head.wait_send()

    loads[3].wait()
    attended = heads[s].astype(BF16)
    wide = 512
    for i in range(width // wide):
        y = jnp.dot(attended, wo_v[:, i * wide : (i + 1) * wide], preferred_element_type=F32)
        for j in range(wide // 128):
            part[i * (wide // 128) + j] = y[:, j * 128 : (j + 1) * 128]

    give_part = duo_copy(4, part, o_rx1)
    give_out = duo_copy(5, g_all, g_all)
    quarter = part.shape[0] // NEAR

    @pl.when(helps)
    def _():
        give_part.start()
        give_part.wait_send()
        give_out.wait_recv()

    @pl.when(leads)
    def _():
        give_part.wait_recv()
        part[...] = part[...] + o_rx1[...]
        copies = loc_copies(
            2,
            lambda place, h: part_of(part, place * quarter, quarter, h),
            lambda i, h: part_of(o_rx2.at[i], 0, quarter, h),
        )
        start(copies)
        stream(1, everyone, next(feeds))
        o_rx2[3] = part[pl.ds(c * quarter, quarter)]
        wait(copies)
        o_tx[...] = (o_rx2[0] + o_rx2[1]) + (o_rx2[2] + o_rx2[3])

        copies = far_copies(3, lambda b: o_tx.at[pl.ds(2 * b, 2)], o_rx3.at[a])
        start(copies)
        stream(1, everyone, next(feeds))
        o_rx3[a] = o_tx[pl.ds(2 * a, 2)]
        wait(copies)
        total = o_rx3[0]
        for i in range(1, SECTIONS):
            total = total + o_rx3[i]
        for e in range(2):
            col = pl.multiple_of((c * quarter + 2 * a + e) * 128, 128)
            g_all[c, a, e] = (hid[:, pl.ds(col, 128)].astype(F32) + total[e]).astype(BF16)

        copies = far_copies(4, lambda b: g_all.at[c, a], g_all.at[c, a])
        start(copies)
        stream(1, everyone, next(feeds))
        wait(copies)

        copies = loc_copies(3, own_g, own_g)
        start(copies)

    stream_rest(1)

    @pl.when(leads)
    def _():
        wait(loc_copies(3, own_g, own_g))
        give_out.start()
        give_out.wait_send()

    give = pltpu.make_async_copy(g_all, g_out, load_sem.at[8])
    give.start()
    keep.wait()
    give.wait()
    for k in everyone:
        piece(k, 0, cols).wait()


def place_kernel(order, recv, g_in, mixed, new, out_sem):
    per_section = ROW_BLOCKS // SECTIONS
    block = recv.shape[2] // per_section
    writes = []
    for i in range(ROW_BLOCKS):
        at = pl.multiple_of(order[i] * block, 128)
        src = recv.at[i // per_section, :, pl.ds((i % per_section) * block, block)]
        copy = pltpu.make_async_copy(src, new.at[:, pl.ds(at, block)], out_sem.at[i])
        copy.start()
        writes.append(copy)
    blocks = g_in.shape[0] * g_in.shape[1] * g_in.shape[2]
    for j in range(blocks):
        mixed[:, j * 128 : (j + 1) * 128] = g_in[
            j // (2 * SECTIONS), (j // 2) % SECTIONS, j % 2
        ]
    for copy in writes:
        copy.wait()


def turn_table():
    half_dim = HEAD_DIM // 2
    freqs = 500000.0 ** (-np.arange(half_dim) * 2.0 / HEAD_DIM)
    steps = np.concatenate([64 * np.arange(HIGH_ROWS), np.arange(64)])
    angles = steps[:, None] * freqs[None, :]
    return np.concatenate([np.cos(angles), np.sin(angles)], -1).astype(np.float32)


def shards(hidden_in, norm_gain, wqkv_old, wo, key_cache, value_cache, lengths, section_order):
    seqs, width = hidden_in.shape
    _, _, rank_cols, rows_old = wqkv_old.shape
    cols = rank_cols // SECTIONS
    block = width // ROW_BLOCKS
    pos_count = key_cache.shape[1]

    vmem = pl.BlockSpec(memory_space=pltpu.VMEM)
    smem = pl.BlockSpec(memory_space=pltpu.SMEM)
    hbm = pl.BlockSpec(memory_space=pl.ANY)
    dma = pltpu.SemaphoreType.DMA
    tile, five = (8, 128), (seqs + 1, 128)
    recv, g_out = pl.pallas_call(
        main_kernel,
        name="stream_and_decode",
        out_shape=(
            pltpu.VMEM((SECTIONS, cols, rows_old), BF16),
            jax.ShapeDtypeStruct((NEAR, SECTIONS, 2, seqs, 128), BF16),
        ),
        in_specs=[hbm, hbm, hbm, smem, smem, hbm, hbm, hbm, hbm],
        out_specs=(vmem, hbm),
        scratch_shapes=[
            pltpu.VMEM((seqs, width), BF16),
            pltpu.VMEM((1, width), F32),
            pltpu.VMEM((HIGH_ROWS + 64, HEAD_DIM), F32),
            pltpu.VMEM((rank_cols, rows_old), BF16),
            pltpu.VMEM(wo.shape, BF16),
            pltpu.VMEM(key_cache.shape, BF16),
            pltpu.VMEM(value_cache.shape, BF16),
            pltpu.VMEM((ROW_BLOCKS, seqs, block), F32),
            pltpu.VMEM((SECTIONS, 2, *five), F32),
            pltpu.VMEM((SECTIONS, 2, *five), F32),
            pltpu.VMEM((2, *tile), BF16),
            pltpu.VMEM((NEAR, SECTIONS, 2, *tile), BF16),
            pltpu.VMEM((seqs, HEADS + 2 * KV_HEADS, HEAD_DIM), F32),
            pltpu.VMEM((NEAR, SECTIONS, 2, *five), F32),
            pltpu.VMEM((NEAR, SECTIONS, 2, *five), F32),
            pltpu.VMEM((NEAR, SECTIONS, 2, *five), F32),
            pltpu.VMEM((NEAR, SECTIONS, 2, *five), F32),
            pltpu.VMEM((SECTIONS, 2, *five), F32),
            pltpu.VMEM((2, seqs, HEAD_DIM), F32),
            pltpu.VMEM((width // 128, seqs, 128), F32),
            pltpu.VMEM((width // 128, seqs, 128), F32),
            pltpu.VMEM((NEAR, width // 512, seqs, 128), F32),
            pltpu.VMEM((width // 512, seqs, 128), F32),
            pltpu.VMEM((SECTIONS, 2, seqs, 128), F32),
            pltpu.VMEM((NEAR, SECTIONS, 2, seqs, 128), BF16),
            dma((9,)),
            dma((SECTIONS,)),
            dma((SECTIONS,)),
            dma((5, SECTIONS)),
            dma((5, SECTIONS)),
            dma((4, NEAR)),
            dma((4, NEAR)),
            dma((6,)),
            dma((6,)),
            pltpu.SemaphoreType.REGULAR((3,)),
            pltpu.SemaphoreType.REGULAR((3,)),
        ],
        compiler_params=pltpu.CompilerParams(collective_id=0, has_side_effects=True),
    )(
        hidden_in,
        norm_gain.reshape(1, width),
        jnp.asarray(turn_table()),
        lengths,
        section_order,
        wqkv_old.reshape(rank_cols, rows_old),
        wo,
        key_cache,
        value_cache,
    )

    mixed_out, new_weight = pl.pallas_call(
        place_kernel,
        name="place",
        out_shape=(
            jax.ShapeDtypeStruct((seqs, width), BF16),
            jax.ShapeDtypeStruct((cols, width), BF16),
        ),
        in_specs=[smem, vmem, vmem],
        out_specs=(vmem, hbm),
        scratch_shapes=[dma((ROW_BLOCKS,))],
    )(section_order, pltpu.with_memory_space_constraint(recv, pltpu.VMEM), g_out)
    return mixed_out, new_weight[None, None]


def solution(mesh):
    placed = (
        P("replica", None),
        P("replica"),
        P(("replica", "tp"), "sub", None, None),
        P(("replica", "tp", "sub"), None),
        P("replica", ("tp", "sub"), None),
        P("replica", ("tp", "sub"), None),
        P("replica"),
        P("replica"),
    )
    return jax.shard_map(
        shards,
        mesh=mesh,
        in_specs=placed,
        out_specs=(P("replica", None), P(("replica", "tp"), "sub", None, None)),
        check_vma=False,
    )
```

profile of v0, /device:TPU:103, one launch (start us, length us, event | category | flops | bytes accessed | tf_op | source)
XLA Modules:
  0.0 272.2 jit_solution(6015390680498747028)
XLA Ops:
  0.6 268.5 %stream_and_decode.1 = (bf16[8,160,1024]{2,1,0:T(8,128)(2,1)S(1)}, bf16[4,8,2,4,128]{4,3,2,1,0:T(4,128)(2,1)}) custom-call(bf16[4,8192]{1,0:T(4,128)(2,1)} %hid_in.1, f32[1,8192]{1,0:T(1,128)} %bitcast.4, f32[136,128]{1,0:T(8,128)} %constant.2.clone.table_in, s32[4]{0:T(128)} %lengths.1, s32[16]{0:T(128)} %order.3, bf16[1280,1024]{1,0:T(8,128)(2,1)} %bitcast.3, ...), custom_call_target="tpu_custom_call" | custom-call | tf_op jit(solution)/shard_map/stream_and_decode/pallas_call | solution.py:516
  269.1 3.1 %place.1 = (bf16[4,8192]{1,0:T(4,128)(2,1)}, bf16[160,8192]{1,0:T(8,128)(2,1)}) custom-call(s32[16]{0:T(128)} %order.3, bf16[8,160,1024]{2,1,0:T(8,128)(2,1)S(1)} %get-tuple-element.6.recv, bf16[4,8,2,4,128]{4,3,2,1,0:T(4,128)(2,1)} %get-tuple-element.7.g_in), custom_call_target="tpu_custom_call" | custom-call | tf_op jit(solution)/shard_map/place/pallas_call | solution.py:576
where the time goes:
time: 273 us; the launch traced here: 272 us
  Pallas kernels  272 us (100%)
    pallas_call x1, Pallas kernels, shards(): pl.pallas_call(main_kernel, name='stream_and_decode', out_shape=(pltpu.VM...  268 us

commit v1 on v0

--- a/solution.py
+++ b/solution.py
@@ -54,9 +54,9 @@
 
 def main_kernel(
     hid_in, gain_in, table_in, lengths, order, w, wo, kc, vc,
-    recv, g_out,
+    recv, g_all,
     hid, gain, table, w_v, wo_v, k_v, v_v, nrm, p_tx, p_rx, q_tx, q_all, rows, state, a_rx1, a_rx2,
-    a_tx, a_rx3, heads, part, o_rx1, o_rx2, o_tx, o_rx3, g_all,
+    a_tx, a_rx3, heads, part, o_rx1, o_rx2, o_tx, o_rx3,
     load_sem, big_s, big_r, far_s, far_r, loc_s, loc_r, duo_s, duo_r, known_lo, known_hi,
 ):
     count = lax.axis_size("tp")
@@ -466,15 +466,12 @@
         give_out.start()
         give_out.wait_send()
 
-    give = pltpu.make_async_copy(g_all, g_out, load_sem.at[8])
-    give.start()
     keep.wait()
-    give.wait()
     for k in everyone:
         piece(k, 0, cols).wait()
 
 
-def place_kernel(order, recv, g_in, mixed, new, out_sem):
+def place_kernel(order, recv, g_in, mixed, new, mixed_v, out_sem):
     per_section = ROW_BLOCKS // SECTIONS
     block = recv.shape[2] // per_section
     writes = []
@@ -486,9 +483,12 @@
         writes.append(copy)
     blocks = g_in.shape[0] * g_in.shape[1] * g_in.shape[2]
     for j in range(blocks):
-        mixed[:, j * 128 : (j + 1) * 128] = g_in[
+        mixed_v[:, j * 128 : (j + 1) * 128] = g_in[
             j // (2 * SECTIONS), (j // 2) % SECTIONS, j % 2
         ]
+    copy = pltpu.make_async_copy(mixed_v, mixed, out_sem.at[ROW_BLOCKS])
+    copy.start()
+    writes.append(copy)
     for copy in writes:
         copy.wait()
 
@@ -513,15 +513,15 @@
     hbm = pl.BlockSpec(memory_space=pl.ANY)
     dma = pltpu.SemaphoreType.DMA
     tile, five = (8, 128), (seqs + 1, 128)
-    recv, g_out = pl.pallas_call(
+    recv, blocks = pl.pallas_call(
         main_kernel,
         name="stream_and_decode",
         out_shape=(
             pltpu.VMEM((SECTIONS, cols, rows_old), BF16),
-            jax.ShapeDtypeStruct((NEAR, SECTIONS, 2, seqs, 128), BF16),
+            pltpu.VMEM((NEAR, SECTIONS, 2, seqs, 128), BF16),
         ),
         in_specs=[hbm, hbm, hbm, smem, smem, hbm, hbm, hbm, hbm],
-        out_specs=(vmem, hbm),
+        out_specs=(vmem, vmem),
         scratch_shapes=[
             pltpu.VMEM((seqs, width), BF16),
             pltpu.VMEM((1, width), F32),
@@ -547,8 +547,7 @@
             pltpu.VMEM((NEAR, width // 512, seqs, 128), F32),
             pltpu.VMEM((width // 512, seqs, 128), F32),
             pltpu.VMEM((SECTIONS, 2, seqs, 128), F32),
-            pltpu.VMEM((NEAR, SECTIONS, 2, seqs, 128), BF16),
-            dma((9,)),
+            dma((8,)),
             dma((SECTIONS,)),
             dma((SECTIONS,)),
             dma((5, SECTIONS)),
@@ -581,9 +580,13 @@
             jax.ShapeDtypeStruct((cols, width), BF16),
         ),
         in_specs=[smem, vmem, vmem],
-        out_specs=(vmem, hbm),
-        scratch_shapes=[dma((ROW_BLOCKS,))],
-    )(section_order, pltpu.with_memory_space_constraint(recv, pltpu.VMEM), g_out)
+        out_specs=(hbm, hbm),
+        scratch_shapes=[pltpu.VMEM((seqs, width), BF16), dma((ROW_BLOCKS + 1,))],
+    )(
+        section_order,
+        pltpu.with_memory_space_constraint(recv, pltpu.VMEM),
+        pltpu.with_memory_space_constraint(blocks, pltpu.VMEM),
+    )
     return mixed_out, new_weight[None, None]
 
 

time: 273 us -> 272 us (level)
  no operation moved by 1% of the time
where the time goes in v1:
time: 272 us; the launch traced here: 271 us
  Pallas kernels  271 us (100%)
    pallas_call x1, Pallas kernels, shards(): pl.pallas_call(main_kernel, name='stream_and_decode', out_shape=(pltpu.VM...  268 us

profile of v1, /device:TPU:103, one launch (start us, length us, event | category | flops | bytes accessed | tf_op | source)
XLA Modules:
  0.0 271.4 jit_solution(15230093644883374893)
XLA Ops:
  0.6 268.5 %stream_and_decode.1 = (bf16[8,160,1024]{2,1,0:T(8,128)(2,1)S(1)}, bf16[4,8,2,4,128]{4,3,2,1,0:T(4,128)(2,1)S(1)}) custom-call(bf16[4,8192]{1,0:T(4,128)(2,1)} %hid_in.1, f32[1,8192]{1,0:T(1,128)} %bitcast.4, f32[136,128]{1,0:T(8,128)} %constant.2.clone.table_in, s32[4]{0:T(128)} %lengths.1, s32[16]{0:T(128)} %order.3, bf16[1280,1024]{1,0:T(8,128)(2,1)} %bitcast.3, ...), custom_call_target="tpu_custom_call" | custom-call | tf_op jit(solution)/shard_map/stream_and_decode/pallas_call | solution.py:516
  269.1 2.3 place.1

commit v2 on v1

--- a/solution.py
+++ b/solution.py
@@ -136,6 +136,7 @@
     feeds = iter(FEEDS)
 
     def stream_rest(core):
+        stream(core, everyone[:5], cols // STEP_ROWS)
         while any(sent.get((core, k), 0) < cols for k in everyone):
             stream(core, everyone, cols // STEP_ROWS)
 

time: 272 us -> 275 us (1.011)
  Pallas kernels: 271 us -> 274 us
    pallas_call x1, Pallas kernels: 268 us -> 272 us  [shards(): pl.pallas_call(main_kernel, name='stream_and_decode', out_shape=(pltpu.VM...]
where the time goes in v2:
time: 275 us
  Pallas kernels  274 us (100%)
    pallas_call x1, Pallas kernels, shards(): pl.pallas_call(main_kernel, name='stream_and_decode', out_shape=(pltpu.VM...  272 us

profile of v2, /device:TPU:103, one launch (start us, length us, event | category | flops | bytes accessed | tf_op | source)
XLA Modules:
  0.0 274.5 jit_solution(1531231157392216717)
XLA Ops:
  0.6 271.6 %stream_and_decode.1 = (bf16[8,160,1024]{2,1,0:T(8,128)(2,1)S(1)}, bf16[4,8,2,4,128]{4,3,2,1,0:T(4,128)(2,1)S(1)}) custom-call(bf16[4,8192]{1,0:T(4,128)(2,1)} %hid_in.1, f32[1,8192]{1,0:T(1,128)} %bitcast.4, f32[136,128]{1,0:T(8,128)} %constant.2.clone.table_in, s32[4]{0:T(128)} %lengths.1, s32[16]{0:T(128)} %order.3, bf16[1280,1024]{1,0:T(8,128)(2,1)} %bitcast.3, ...), custom_call_target="tpu_custom_call" | custom-call | tf_op jit(solution)/shard_map/stream_and_decode/pallas_call | solution.py:517
  272.2 2.3 place.1
